TPU v7x, 256 devices: a whole 4x4x8 slice. The times are simulated.
256 devices in a mesh: row: 16 (over z_hi, x), col: 16 (over y, z_lo, core).
Axes of the slice: x: 4, y: 4, z: 8 (z_hi: 4, z_lo: 2; z = z_hi * 2 + z_lo), core: 2. Of those that a mesh axis runs over, the one named last changes fastest.
Arguments:
- gradients: bfloat16 [256, 2, 524288], P(('row', 'col')), may hold values from -384 to 384
- master_params: float32 [2, 524288], P(None, ('row', 'col')), may hold values from -0.1 to 0.1
- first_moment: float32 [2, 524288], P(None, ('row', 'col')), may hold values from -3 to 3
- second_moment: float32 [2, 524288], P(None, ('row', 'col')), may hold values from 0.05 to 5
Outputs:
- new_master: float32 [2, 524288], P(None, ('row', 'col'))
- new_first: float32 [2, 524288], P(None, ('row', 'col'))
- new_second: float32 [2, 524288], P(None, ('row', 'col'))
- new_weights: bfloat16 [2, 524288], replicated
All inputs are finite; a program needn't handle non-finite values.
Results may differ from a plain program's by a relative error of at most 0.009.
Values may be sent and summed in bfloat16 or wider, within the bound.
A program may use at most 64 MiB of HBM per device.

v0:
```python
import jax
import jax.numpy as jnp
from jax import lax
from jax.sharding import PartitionSpec as P

beta_one = 0.9
beta_two = 0.95
learn_rate = 0.001
decay_rate = 0.1
epsilon = 1e-08
adam_step = 10.0


def in_blocks(shard, dim, length):
    lengths = shard.shape
    pieces = shard.reshape(*lengths[:dim], length, lengths[dim] // length, *lengths[dim + 1 :])
    return jnp.moveaxis(pieces, dim, 0)


def summed_on_arrival(shard, axis, dim):
    pieces = in_blocks(shard, dim, lax.axis_size(axis))
    arrived = lax.all_to_all(pieces, axis, split_axis=0, concat_axis=0, tiled=True)
    return arrived.astype(jnp.float32).sum(axis=0)


def laid_out(pieces, dim):
    lengths = list(pieces.shape[1:])
    lengths[dim] *= pieces.shape[0]
    return jnp.moveaxis(pieces, 0, dim).reshape(lengths)


def from_everyone(shard, axis):
    length = lax.axis_size(axis)
    return lax.all_to_all(
        jnp.broadcast_to(shard[None], (length, *shard.shape)), axis, 0, 0, tiled=True
    )


def gathered_copies(shard, axis, dim):
    return laid_out(from_everyone(shard, axis), dim)


def adam_update(mean_grad, master_params, first_moment, second_moment):
    new_first = beta_one * first_moment + (1.0 - beta_one) * mean_grad
    new_second = beta_two * second_moment + (1.0 - beta_two) * mean_grad * mean_grad
    first_hat = new_first / (1.0 - beta_one**adam_step)
    second_hat = new_second / (1.0 - beta_two**adam_step)
    new_master = master_params - learn_rate * (
        first_hat / (jnp.sqrt(second_hat) + epsilon) + decay_rate * master_params
    )
    return (new_master, new_first, new_second)


def shards(gradients, master_params, first_moment, second_moment):
    row_count = lax.axis_size("row")
    col_count = lax.axis_size("col")
    slice_len = gradients.shape[2]
    portion = slice_len // (row_count * col_count)
    summed_grad = gradients[0].astype(jnp.float32)
    former = summed_grad[0].reshape(row_count, col_count, portion)
    latter = summed_grad[1].reshape(row_count, col_count, portion)
    former = summed_on_arrival(former.astype(jnp.bfloat16), "row", 0)
    latter = summed_on_arrival(latter.astype(jnp.bfloat16), "col", 1)
    former = summed_on_arrival(former.astype(jnp.bfloat16), "col", 1)
    latter = summed_on_arrival(latter.astype(jnp.bfloat16), "row", 0)
    reduced = jnp.stack([former.reshape(portion), latter.reshape(portion)])
    mean_grad = reduced / (row_count * col_count)
    new_master, new_first, new_second = adam_update(
        mean_grad, master_params, first_moment, second_moment
    )
    rounded = new_master.astype(jnp.bfloat16)
    former_w = rounded[0].reshape(1, 1, portion)
    latter_w = rounded[1].reshape(1, 1, portion)
    former_w = gathered_copies(former_w, "col", 1)
    latter_w = gathered_copies(latter_w, "row", 0)
    former_w = gathered_copies(former_w, "row", 0)
    latter_w = gathered_copies(latter_w, "col", 1)
    new_weights = jnp.stack([former_w.reshape(slice_len), latter_w.reshape(slice_len)])
    return (new_master, new_first, new_second, new_weights)


def solution(mesh):
    in_specs = (
        P(("row", "col"), None, None),
        P(None, ("row", "col")),
        P(None, ("row", "col")),
        P(None, ("row", "col")),
    )
    out_specs = (P(None, ("row", "col")), P(None, ("row", "col")), P(None, ("row", "col")), P())
    return jax.shard_map(shards, mesh=mesh, in_specs=in_specs, out_specs=out_specs, check_vma=False)
```

profile of v0, /device:TPU:32, one launch (start us, length us, event | category | flops | bytes accessed | tf_op | source)
XLA Modules:
  0.0 202.2 jit_solution(2868079000624234701)
XLA Ops:
  0.6 23.7 %slice_reduce_fusion.1 = (bf16[524288]{0:T(1024)(128)(2,1)S(1)}, bf16[524288]{0:T(1024)(128)(2,1)S(1)}) fusion(bf16[1,2,524288]{2,1,0:T(2,128)(2,1)} %param.4), kind=kLoop, calls=%fused_computation.2 | loop fusion | bytes 4194304 | tf_op jit(solution)/shard_map/slice | solution.py:60
  24.3 1.3 convert_element_type.39
  25.6 10.1 %all-to-all-start = ((bf16[16,1,16,2048]{3,2,1,0:T(8,128)(2,1)}), bf16[16,1,16,2048]{3,2,1,0:T(8,128)(2,1)S(1)}, u32[]{:S(2)}, u32[]{:S(2)}) async-start(bf16[16,1,16,2048]{3,2,1,0:T(8,128)(2,1)} %convert_element_type.39), calls=%async_computation | async-start | bytes 2097152 | tf_op jit(solution)/shard_map/all_to_all | solution.py:22
  35.7 0.5 convert_element_type.41
  36.2 1.5 copy.9
  37.8 27.1 %all-to-all-done = bf16[16,1,16,2048]{3,2,1,0:T(8,128)(2,1)S(1)} async-done(((bf16[16,1,16,2048]{3,2,1,0:T(8,128)(2,1)}), bf16[16,1,16,2048]{3,2,1,0:T(8,128)(2,1)S(1)}, u32[]{:S(2)}, u32[]{:S(2)}) %all-to-all-start) | async-done | bytes 1048608 | tf_op jit(solution)/shard_map/all_to_all | solution.py:22
  64.9 5.9 %all-to-all-start.2 = ((bf16[16,16,1,2048]{3,1,2,0:T(8,128)(2,1)}), bf16[16,16,1,2048]{3,1,2,0:T(8,128)(2,1)S(1)}, u32[]{:S(2)}, u32[]{:S(2)}) async-start(bf16[16,16,1,2048]{3,1,2,0:T(8,128)(2,1)} %copy.9), calls=%async_computation.2 | async-start | bytes 2097152 | tf_op jit(solution)/shard_map/all_to_all | solution.py:22
  70.8 0.0 copy-start.1
  70.8 0.1 reduce_sum.42
  71.0 0.5 broadcast.19
  71.5 0.6 reduce.15
  72.2 0.7 reshape.69
  72.8 13.3 %all-to-all-done.2 = bf16[16,16,1,2048]{3,1,2,0:T(8,128)(2,1)S(1)} async-done(((bf16[16,16,1,2048]{3,1,2,0:T(8,128)(2,1)}), bf16[16,16,1,2048]{3,1,2,0:T(8,128)(2,1)S(1)}, u32[]{:S(2)}, u32[]{:S(2)}) %all-to-all-start.2) | async-done | bytes 1048608 | tf_op jit(solution)/shard_map/all_to_all | solution.py:22
  86.1 4.6 %all-to-all-start.1 = ((bf16[16,2,1024]{2,1,0:T(2,128)(2,1)}), bf16[16,2,1024]{2,1,0:T(2,128)(2,1)S(1)}, u32[]{:S(2)}, u32[]{:S(2)}) async-start(bf16[16,2,1024]{2,1,0:T(2,128)(2,1)} %reshape.69), calls=%async_computation.1 | async-start | bytes 131072 | tf_op jit(solution)/shard_map/all_to_all | solution.py:22
  90.7 0.1 reduce_sum.44
  90.9 0.6 reduce.14
  91.5 0.7 reshape.67
  92.2 3.5 %all-to-all-done.1 = bf16[16,2,1024]{2,1,0:T(2,128)(2,1)S(1)} async-done(((bf16[16,2,1024]{2,1,0:T(2,128)(2,1)}), bf16[16,2,1024]{2,1,0:T(2,128)(2,1)S(1)}, u32[]{:S(2)}, u32[]{:S(2)}) %all-to-all-start.1) | async-done | bytes 65568 | tf_op jit(solution)/shard_map/all_to_all | solution.py:22
  95.6 4.2 %all-to-all-start.3 = ((bf16[16,2,1024]{2,1,0:T(2,128)(2,1)}), bf16[16,2,1024]{2,1,0:T(2,128)(2,1)S(1)}, u32[]{:S(2)}, u32[]{:S(2)}) async-start(bf16[16,2,1024]{2,1,0:T(2,128)(2,1)} %reshape.67), calls=%async_computation.3 | async-start | bytes 131072 | tf_op jit(solution)/shard_map/all_to_all | solution.py:22
  99.9 0.1 reshape.70
  100.0 0.1 convert_reduce_fusion.1
  100.1 9.9 %all-to-all-done.3 = bf16[16,2,1024]{2,1,0:T(2,128)(2,1)S(1)} async-done(((bf16[16,2,1024]{2,1,0:T(2,128)(2,1)}), bf16[16,2,1024]{2,1,0:T(2,128)(2,1)S(1)}, u32[]{:S(2)}, u32[]{:S(2)}) %all-to-all-start.3) | async-done | bytes 65568 | tf_op jit(solution)/shard_map/all_to_all | solution.py:22
  110.0 0.1 reshape.68
  110.1 0.1 convert_reduce_fusion
  110.2 0.7 fusion
  110.9 0.1 slice_reduce_fusion.3
  111.0 0.1 broadcast_in_dim.33
  111.0 1.0 reduce.16
  112.0 0.7 reshape.71
  112.7 3.5 %all-to-all-start.6 = ((bf16[16,2,1024]{2,1,0:T(2,128)(2,1)}), bf16[16,2,1024]{2,1,0:T(2,128)(2,1)S(1)}, u32[]{:S(2)}, u32[]{:S(2)}) async-start(bf16[16,2,1024]{2,1,0:T(2,128)(2,1)} %reshape.71), calls=%async_computation.6 | async-start | bytes 131072 | tf_op jit(solution)/shard_map/all_to_all | solution.py:34
  116.2 0.1 broadcast_in_dim.29
  116.3 1.0 reduce.17
  117.2 0.7 reshape.73
  117.9 8.4 %all-to-all-done.6 = bf16[16,2,1024]{2,1,0:T(2,128)(2,1)S(1)} async-done(((bf16[16,2,1024]{2,1,0:T(2,128)(2,1)}), bf16[16,2,1024]{2,1,0:T(2,128)(2,1)S(1)}, u32[]{:S(2)}, u32[]{:S(2)}) %all-to-all-start.6) | async-done | bytes 65568 | tf_op jit(solution)/shard_map/all_to_all | solution.py:34
  126.2 4.7 %all-to-all-start.4 = ((bf16[16,2,1024]{2,1,0:T(2,128)(2,1)}), bf16[16,2,1024]{2,1,0:T(2,128)(2,1)S(1)}, u32[]{:S(2)}, u32[]{:S(2)}) async-start(bf16[16,2,1024]{2,1,0:T(2,128)(2,1)} %reshape.73), calls=%async_computation.4 | async-start | bytes 131072 | tf_op jit(solution)/shard_map/all_to_all | solution.py:34
  130.9 0.1 reshape.72
  131.0 4.8 %all-to-all-done.4 = bf16[16,2,1024]{2,1,0:T(2,128)(2,1)S(1)} async-done(((bf16[16,2,1024]{2,1,0:T(2,128)(2,1)}), bf16[16,2,1024]{2,1,0:T(2,128)(2,1)S(1)}, u32[]{:S(2)}, u32[]{:S(2)}) %all-to-all-start.4) | async-done | bytes 65568 | tf_op jit(solution)/shard_map/all_to_all | solution.py:34
  135.8 1.1 broadcast_in_dim.35
  136.9 4.8 %all-to-all-start.7 = ((bf16[16,16,1,2048]{3,1,2,0:T(8,128)(2,1)}), bf16[16,16,1,2048]{3,1,2,0:T(8,128)(2,1)S(1)}, u32[]{:S(2)}, u32[]{:S(2)}) async-start(bf16[16,16,1,2048]{3,1,2,0:T(8,128)(2,1)} %broadcast_in_dim.35), calls=%async_computation.7 | async-start | bytes 2097152 | tf_op jit(solution)/shard_map/all_to_all | solution.py:34
  141.8 0.1 reshape.74
  141.9 15.3 %all-to-all-done.7 = bf16[16,16,1,2048]{3,1,2,0:T(8,128)(2,1)S(1)} async-done(((bf16[16,16,1,2048]{3,1,2,0:T(8,128)(2,1)}), bf16[16,16,1,2048]{3,1,2,0:T(8,128)(2,1)S(1)}, u32[]{:S(2)}, u32[]{:S(2)}) %all-to-all-start.7) | async-done | bytes 1048608 | tf_op jit(solution)/shard_map/all_to_all | solution.py:34
  157.1 1.1 broadcast_in_dim.31
  158.2 3.8 %all-to-all-start.5 = ((bf16[16,1,16,2048]{3,2,1,0:T(8,128)(2,1)}), bf16[16,1,16,2048]{3,2,1,0:T(8,128)(2,1)S(1)}, u32[]{:S(2)}, u32[]{:S(2)}) async-start(bf16[16,1,16,2048]{3,2,1,0:T(8,128)(2,1)} %broadcast_in_dim.31), calls=%async_computation.5 | async-start | bytes 2097152 | tf_op jit(solution)/shard_map/all_to_all | solution.py:34
  162.1 0.6 copy.11
  162.6 1.6 copy.14
  164.3 28.7 %all-to-all-done.5 = bf16[16,1,16,2048]{3,2,1,0:T(8,128)(2,1)S(1)} async-done(((bf16[16,1,16,2048]{3,2,1,0:T(8,128)(2,1)}), bf16[16,1,16,2048]{3,2,1,0:T(8,128)(2,1)S(1)}, u32[]{:S(2)}, u32[]{:S(2)}) %all-to-all-start.5) | async-done | bytes 1048608 | tf_op jit(solution)/shard_map/all_to_all | solution.py:34
  192.9 2.7 %stack_reshape_reshape.6 = bf16[1,524288]{1,0:T(2,128)(2,1)} reshape(bf16[16,1,16,2048]{3,2,1,0:T(8,128)(2,1)S(1)} %all-to-all-done.5) | data formatting | bytes 2097152 | tf_op jit(solution)/shard_map/stack;reshape;reshape | solution.py:78
  195.6 6.7 %pad_maximum_fusion = bf16[2,524288]{1,0:T(2,128)(2,1)} fusion(bf16[1,524288]{1,0:T(2,128)(2,1)S(1)} %bitcast.18, bf16[1,524288]{1,0:T(2,128)(2,1)} %stack_reshape_reshape.6), kind=kLoop, calls=%fused_computation | loop fusion | flops 4194304 | bytes 4194304 | tf_op jit(solution)/shard_map/stack | solution.py:78
  (7 shorter events, 0.1 us)
Async XLA Ops:
  25.6 39.3 %all-to-all-start = ((bf16[16,1,16,2048]{3,2,1,0:T(8,128)(2,1)}), bf16[16,1,16,2048]{3,2,1,0:T(8,128)(2,1)S(1)}, u32[]{:S(2)}, u32[]{:S(2)}) async-start(bf16[16,1,16,2048]{3,2,1,0:T(8,128)(2,1)} %convert_element_type.39), calls=%async_computation | async-start | bytes 2097152 | tf_op jit(solution)/shard_map/all_to_all | solution.py:22
  64.9 21.3 %all-to-all-start.2 = ((bf16[16,16,1,2048]{3,1,2,0:T(8,128)(2,1)}), bf16[16,16,1,2048]{3,1,2,0:T(8,128)(2,1)S(1)}, u32[]{:S(2)}, u32[]{:S(2)}) async-start(bf16[16,16,1,2048]{3,1,2,0:T(8,128)(2,1)} %copy.9), calls=%async_computation.2 | async-start | bytes 2097152 | tf_op jit(solution)/shard_map/all_to_all | solution.py:22
  70.8 39.4 %copy-start = (f32[2,2048]{1,0:T(2,128)S(1)}, f32[2,2048]{1,0:T(2,128)}, u32[]{:S(2)}) copy-start(f32[2,2048]{1,0:T(2,128)} %param.5) | copy-start | bytes 49156
  70.8 39.4 %copy-start.1 = (f32[2,2048]{1,0:T(2,128)S(1)}, f32[2,2048]{1,0:T(2,128)}, u32[]{:S(2)}) copy-start(f32[2,2048]{1,0:T(2,128)} %param.6) | copy-start | bytes 49156
  70.8 39.4 %copy-start.2 = (f32[2,2048]{1,0:T(2,128)S(1)}, f32[2,2048]{1,0:T(2,128)}, u32[]{:S(2)}) copy-start(f32[2,2048]{1,0:T(2,128)} %param.7) | copy-start | bytes 49156
  86.1 9.5 %all-to-all-start.1 = ((bf16[16,2,1024]{2,1,0:T(2,128)(2,1)}), bf16[16,2,1024]{2,1,0:T(2,128)(2,1)S(1)}, u32[]{:S(2)}, u32[]{:S(2)}) async-start(bf16[16,2,1024]{2,1,0:T(2,128)(2,1)} %reshape.69), calls=%async_computation.1 | async-start | bytes 131072 | tf_op jit(solution)/shard_map/all_to_all | solution.py:22
  95.6 14.4 %all-to-all-start.3 = ((bf16[16,2,1024]{2,1,0:T(2,128)(2,1)}), bf16[16,2,1024]{2,1,0:T(2,128)(2,1)S(1)}, u32[]{:S(2)}, u32[]{:S(2)}) async-start(bf16[16,2,1024]{2,1,0:T(2,128)(2,1)} %reshape.67), calls=%async_computation.3 | async-start | bytes 131072 | tf_op jit(solution)/shard_map/all_to_all | solution.py:22
  112.7 13.6 %all-to-all-start.6 = ((bf16[16,2,1024]{2,1,0:T(2,128)(2,1)}), bf16[16,2,1024]{2,1,0:T(2,128)(2,1)S(1)}, u32[]{:S(2)}, u32[]{:S(2)}) async-start(bf16[16,2,1024]{2,1,0:T(2,128)(2,1)} %reshape.71), calls=%async_computation.6 | async-start | bytes 131072 | tf_op jit(solution)/shard_map/all_to_all | solution.py:34
  126.2 9.6 %all-to-all-start.4 = ((bf16[16,2,1024]{2,1,0:T(2,128)(2,1)}), bf16[16,2,1024]{2,1,0:T(2,128)(2,1)S(1)}, u32[]{:S(2)}, u32[]{:S(2)}) async-start(bf16[16,2,1024]{2,1,0:T(2,128)(2,1)} %reshape.73), calls=%async_computation.4 | async-start | bytes 131072 | tf_op jit(solution)/shard_map/all_to_all | solution.py:34
  136.9 20.2 %all-to-all-start.7 = ((bf16[16,16,1,2048]{3,1,2,0:T(8,128)(2,1)}), bf16[16,16,1,2048]{3,1,2,0:T(8,128)(2,1)S(1)}, u32[]{:S(2)}, u32[]{:S(2)}) async-start(bf16[16,16,1,2048]{3,1,2,0:T(8,128)(2,1)} %broadcast_in_dim.35), calls=%async_computation.7 | async-start | bytes 2097152 | tf_op jit(solution)/shard_map/all_to_all | solution.py:34
  158.2 34.7 %all-to-all-start.5 = ((bf16[16,1,16,2048]{3,2,1,0:T(8,128)(2,1)}), bf16[16,1,16,2048]{3,2,1,0:T(8,128)(2,1)S(1)}, u32[]{:S(2)}, u32[]{:S(2)}) async-start(bf16[16,1,16,2048]{3,2,1,0:T(8,128)(2,1)} %broadcast_in_dim.31), calls=%async_computation.5 | async-start | bytes 2097152 | tf_op jit(solution)/shard_map/all_to_all | solution.py:34
where the time goes:
time: 203 us; the launch traced here: 202 us
  waiting for transfers between devices  111 us (55%)
  starting transfers between devices  41.8 us (21%)
  local copies, waits for them, and re-layouts  37.7 us (19%)
  other arithmetic  11.1 us (5%)
    all_to_all x4, waiting for transfers between devices, from_everyone(): lax.all_to_all(jnp.broadcast_to(shard[None], (length, *shard.shape)), axi...  57.1 us
    all_to_all x4, waiting for transfers between devices, summed_on_arrival(): lax.all_to_all(pieces, axis, split_axis=0, concat_axis=0, tiled=True)  53.8 us
    all_to_all x4, starting transfers between devices, summed_on_arrival(): lax.all_to_all(pieces, axis, split_axis=0, concat_axis=0, tiled=True)  24.9 us
    slice x1, local copies, waits for them, and re-layouts, shards(): former = summed_grad[0].reshape(row_count, col_count, portion)  23.7 us
    all_to_all x4, starting transfers between devices, from_everyone(): lax.all_to_all(jnp.broadcast_to(shard[None], (length, *shard.shape)), axi...  16.8 us
    another operation x1, other arithmetic, shards(): jnp.stack([former_w.reshape(slice_len), latter_w.reshape(slice_len)])  6.66 us
    unnamed x17, local copies, waits for them, and re-layouts  4.55 us
  transfers between devices with their start and end apart: 8, of which 8 were waited for; matrix products, arithmetic and copies ran while one was open for 5% of the time, Pallas kernels for 0%

commit v1 on v0

v1 whole, which is shorter than its diff:
```python
import jax
import jax.numpy as jnp
from jax import lax
from jax.experimental import pallas as pl
from jax.experimental.pallas import tpu as pltpu
from jax.sharding import PartitionSpec as P

beta_one = 0.9
beta_two = 0.95
learn_rate = 0.001
decay_rate = 0.1
epsilon = 1e-08
adam_step = 10.0

MESH = pl.DeviceIdType.MESH
F32 = jnp.float32
BF16 = jnp.bfloat16

PIECES = ((2, 0), (2, 1), (1, 1), (3, 0), (1, 0), (3, 1), (0, 0), (0, 1))


def adam_update(mean_grad, master_params, first_moment, second_moment):
    new_first = beta_one * first_moment + (1.0 - beta_one) * mean_grad
    new_second = beta_two * second_moment + (1.0 - beta_two) * mean_grad * mean_grad
    first_hat = new_first / (1.0 - beta_one**adam_step)
    second_hat = new_second / (1.0 - beta_two**adam_step)
    new_master = master_params - learn_rate * (
        first_hat / (jnp.sqrt(second_hat) + epsilon) + decay_rate * master_params
    )
    return (new_master, new_first, new_second)


def mod(value, size):
    return lax.rem(value, size)


def kernel(
    g, master, first, second,
    new_master, new_first, new_second, weights,
    own, given, sent1, got1, sum1, sent2, got2, sum2, got3, mine, theirs,
    load_sem, send0, recv0, send1, recv1, send2, recv2, send3, recv3,
    send4, recv4, send5, recv5, send6, recv6, send7, recv7, out_sem,
):
    row = lax.axis_index("row")
    col = lax.axis_index("col")
    z_hi = lax.div(row, 4)
    x = mod(row, 4)
    y = lax.div(col, 4)
    z_lo = mod(lax.div(col, 2), 2)
    core = mod(col, 2)
    z = z_hi * 2 + z_lo
    a = x + core * (y - x)
    b = y + core * (x - y)

    def device(a_of, b_of, z_of):
        x_of = a_of + core * (b_of - a_of)
        y_of = b_of + core * (a_of - b_of)
        return (lax.div(z_of, 2) * 4 + x_of, y_of * 4 + mod(z_of, 2) * 2 + core)

    partner = (row, col + 1 - 2 * core)
    a_right, a_left = device(mod(a + 1, 4), b, z), device(mod(a + 3, 4), b, z)
    b_right, b_left = device(a, mod(b + 1, 4), z), device(a, mod(b + 3, 4), z)
    along_z = [None] + [device(a, b, mod(z + k, 8)) for k in range(1, 8)]

    def remote(source, target, send_sem, recv_sem, where):
        return pltpu.make_async_remote_copy(
            src_ref=source, dst_ref=target, send_sem=send_sem, recv_sem=recv_sem,
            device_id=where, device_id_type=MESH,
        )

    barrier = pltpu.get_barrier_semaphore()
    peers = [partner, a_right, a_left, b_right, b_left] + along_z[1:]
    for peer in peers:
        pl.semaphore_signal(barrier, inc=1, device_id=peer, device_id_type=MESH)

    def part_of(core_v, place, half):
        zs = pl.ds(2 * half, 2)
        if core_v == 0:
            return (zs, place, slice(None), slice(None), 0)
        return (zs, slice(None), place, slice(None), 1)

    for core_v in (0, 1):
        @pl.when(core == core_v)
        def _():
            for k, (off, half) in enumerate(PIECES):
                source = g.at[part_of(core_v, mod(a + off, 4), half)]
                pltpu.make_async_copy(source, own.at[k], load_sem.at[k]).start()

    pl.semaphore_wait(barrier, len(peers))

    for core_v in (0, 1):
        @pl.when(core == core_v)
        def _():
            for k, (off, half) in enumerate(PIECES):
                source = g.at[part_of(1 - core_v, mod(b + off, 4), half)]
                remote(source, given.at[k], send0.at[k], recv0.at[k], partner).start()

    def piece_ready(k):
        pltpu.make_async_copy(own.at[k], own.at[k], load_sem.at[k]).wait()
        remote(own.at[k], given.at[k], send0.at[k], recv0.at[k], partner).wait_recv()

    def add_up(count, parts, store):
        def step(i, _):
            total = parts[0](i).astype(F32)
            for part in parts[1:]:
                total = total + part(i).astype(F32)
            store(i, total)
            return 0
        lax.fori_loop(0, count, step, 0)

    def block8(ref, k):
        return lambda i: ref[k, lax.div(i, 4), mod(i, 4)]

    def into_block8(ref, k):
        def store(i, value):
            ref[k, lax.div(i, 4), mod(i, 4)] = value.astype(BF16)
        return store

    to1 = (a_right, a_left, a_right, a_left, a_right, a_left)

    def ring1(k):
        return remote(sent1.at[k], got1.at[k], send1.at[k], recv1.at[k], to1[k])

    for k in range(4):
        piece_ready(k)
        add_up(8, [block8(own, k), block8(given, k)], into_block8(sent1, k))
        ring1(k).start()
    for k in (4, 5):
        piece_ready(k)
        ring1(k - 4).wait_recv()
        add_up(
            8, [block8(own, k), block8(given, k), block8(got1, k - 4)], into_block8(sent1, k)
        )
        ring1(k).start()
    piece_ready(6)
    piece_ready(7)

    def into_sum1(half):
        def store(i, value):
            sum1[mod(i, 4), 2 * half + lax.div(i, 4)] = value.astype(BF16)
        return store

    for half, (early, late) in enumerate(((3, 4), (2, 5))):
        ring1(early).wait_recv()
        ring1(late).wait_recv()
        add_up(
            8,
            [block8(own, 6 + half), block8(given, 6 + half), block8(got1, early), block8(got1, late)],
            into_sum1(half),
        )

    b_1, b_2, b_3 = mod(b + 1, 4), mod(b + 2, 4), mod(b + 3, 4)
    to2 = (b_right, b_left, b_right, b_left, b_right, b_left)

    def half2(place, half):
        return sum1.at[place, pl.ds(2 * half, 2)]

    from2 = (half2(b_2, 0), half2(b_2, 1), half2(b_1, 1), half2(b_3, 0), sent2.at[0], sent2.at[1])

    def ring2(k):
        return remote(from2[k], got2.at[k], send2.at[k], recv2.at[k], to2[k])

    for k in range(4):
        ring2(k).start()
    for k, (place, half) in ((4, (b_1, 0)), (5, (b_3, 1))):
        ring2(k - 4).wait_recv()
        def store(i, value):
            sent2[k - 4, i] = value.astype(BF16)
        add_up(
            2, [lambda i: sum1[place, 2 * half + i], lambda i: got2[k - 4, i]], store
        )
        ring2(k).start()
    for half, (early, late) in enumerate(((3, 4), (2, 5))):
        ring2(early).wait_recv()
        ring2(late).wait_recv()
        def store(i, value):
            sum2[2 * half + i] = value.astype(BF16)
        add_up(
            2,
            [lambda i: sum1[b, 2 * half + i], lambda i: got2[early, i], lambda i: got2[late, i]],
            store,
        )

    def across(k):
        z_of = mod(z + k, 8)
        return remote(
            sum2.at[lax.div(z_of, 2), mod(z_of, 2)], got3.at[k], send3.at[k], recv3.at[k], along_z[k]
        )

    order = (4, 3, 5, 2, 6, 1, 7)
    for k in order:
        across(k).start()
    total = sum2[z_hi, z_lo].astype(F32)
    for k in (1, 7, 2, 6, 3, 5, 4):
        across(k).wait_recv()
        total = total + got3[k].astype(F32)
    mean_grad = total / 256.0
    m_new, f_new, s_new = adam_update(mean_grad, master[...], first[...], second[...])
    new_master[...] = m_new
    new_first[...] = f_new
    new_second[...] = s_new
    mine[a, z_hi, b, z_lo] = m_new.astype(BF16)

    def gather_z(k):
        here = mine.at[a, z_hi, b, z_lo]
        return remote(here, here, send4.at[k], recv4.at[k], along_z[k])

    for k in order:
        gather_z(k).start()
    for k in (1, 7, 2, 6, 3, 5, 4):
        gather_z(k).wait_recv()

    def half5(place, half):
        return mine.at[a, pl.ds(2 * half, 2), place]

    send_what5 = ((b, 0), (b, 1), (b_3, 0), (b, 1), (b, 0), (b_1, 1))

    def gather_b(k):
        piece = half5(*send_what5[k])
        return remote(piece, piece, send5.at[k], recv5.at[k], b_right if k < 3 else b_left)

    for k in (0, 3, 1, 4):
        gather_b(k).start()
    gather_b(0).wait_recv()
    gather_b(2).start()
    gather_b(3).wait_recv()
    gather_b(5).start()
    for k in (1, 4, 2, 5):
        gather_b(k).wait_recv()

    a_1, a_2, a_3 = mod(a + 1, 4), mod(a + 2, 4), mod(a + 3, 4)

    def half6(ref, place, half):
        return ref.at[place, pl.ds(2 * half, 2)]

    send_what6 = ((a, 0), (a, 1), (a_3, 0), (a, 1), (a, 0), (a_1, 1))

    def gather_a(k):
        piece = half6(mine, *send_what6[k])
        return remote(piece, piece, send6.at[k], recv6.at[k], a_right if k < 3 else a_left)

    final = ((0, 0), (0, 1), (3, 0), (1, 1), (3, 1), (1, 0), (2, 0), (2, 1))

    def pass_on(j):
        off, half = final[j]
        place = mod(a + off, 4)
        return remote(
            half6(mine, place, half), half6(theirs, place, half), send7.at[j], recv7.at[j], partner
        )

    def write(j, from_partner):
        off, half = final[j]
        sem = out_sem.at[j + 8 * from_partner]
        for core_v in (0, 1):
            @pl.when(core == core_v)
            def _():
                if from_partner:
                    place = mod(b + off, 4)
                    pltpu.make_async_copy(
                        half6(theirs, place, half), weights.at[part_of(1 - core_v, place, half)], sem
                    ).start()
                else:
                    place = mod(a + off, 4)
                    pltpu.make_async_copy(
                        half6(mine, place, half), weights.at[part_of(core_v, place, half)], sem
                    ).start()

    for k in (0, 3, 1, 4):
        gather_a(k).start()
    pass_on(0).start()
    pass_on(1).start()
    write(0, 0)
    write(1, 0)
    for k, follow, j in ((0, 2, 2), (3, 5, 3), (1, None, 4), (4, None, 5), (2, None, 6), (5, None, 7)):
        gather_a(k).wait_recv()
        if follow is not None:
            gather_a(follow).start()
        pass_on(j).start()
        write(j, 0)
    for j in range(8):
        pass_on(j).wait_recv()
        write(j, 1)

    for k in range(8):
        remote(own.at[k], given.at[k], send0.at[k], recv0.at[k], partner).wait_send()
        pass_on(k).wait_send()
    for k in range(6):
        ring1(k).wait_send()
        ring2(k).wait_send()
        gather_b(k).wait_send()
        gather_a(k).wait_send()
    for k in range(1, 8):
        across(k).wait_send()
        gather_z(k).wait_send()
    for j in range(16):
        pltpu.make_async_copy(own.at[0], own.at[0], out_sem.at[j]).wait()


def as_rows(array):
    columns = array.shape[1]
    return array.reshape(2, columns // 128, 128).transpose(1, 0, 2).reshape(columns // 64, 128)


def from_rows(array):
    rows = array.shape[0]
    return array.reshape(rows // 2, 2, 128).transpose(1, 0, 2).reshape(2, rows * 64)


def shards(gradients, master_params, first_moment, second_moment):
    g = as_rows(gradients[0]).reshape(4, 4, 4, 2, 2, 32, 128)
    small = [as_rows(array) for array in (master_params, first_moment, second_moment)]
    dma = pltpu.SemaphoreType.DMA
    block = (2, 4, 2, 32, 128)
    vmem = pl.BlockSpec(memory_space=pltpu.VMEM)
    outs = pl.pallas_call(
        kernel,
        out_shape=[jax.ShapeDtypeStruct((32, 128), F32)] * 3
        + [jax.ShapeDtypeStruct(g.shape, BF16)],
        in_specs=[pl.BlockSpec(memory_space=pltpu.HBM)] + [vmem] * 3,
        out_specs=[vmem] * 3 + [pl.BlockSpec(memory_space=pltpu.HBM)],
        scratch_shapes=[
            pltpu.VMEM((8, *block), BF16),
            pltpu.VMEM((8, *block), BF16),
            pltpu.VMEM((6, *block), BF16),
            pltpu.VMEM((6, *block), BF16),
            pltpu.VMEM((4, 4, 2, 32, 128), BF16),
            pltpu.VMEM((2, 2, 2, 32, 128), BF16),
            pltpu.VMEM((6, 2, 2, 32, 128), BF16),
            pltpu.VMEM((4, 2, 32, 128), BF16),
            pltpu.VMEM((8, 32, 128), BF16),
            pltpu.VMEM((4, 4, 4, 2, 32, 128), BF16),
            pltpu.VMEM((4, 4, 4, 2, 32, 128), BF16),
            dma((8,)),
            dma((8,)), dma((8,)),
            dma((6,)), dma((6,)),
            dma((6,)), dma((6,)),
            dma((8,)), dma((8,)),
            dma((8,)), dma((8,)),
            dma((6,)), dma((6,)),
            dma((6,)), dma((6,)),
            dma((8,)), dma((8,)),
            dma((16,)),
        ],
        compiler_params=pltpu.CompilerParams(collective_id=0, has_side_effects=True),
        name="average_and_update",
    )(g, *small)
    new_master, new_first, new_second = [from_rows(array) for array in outs[:3]]
    return (new_master, new_first, new_second, from_rows(outs[3].reshape(8192, 128)))


def solution(mesh):
    in_specs = (
        P(("row", "col"), None, None),
        P(None, ("row", "col")),
        P(None, ("row", "col")),
        P(None, ("row", "col")),
    )
    out_specs = (P(None, ("row", "col")), P(None, ("row", "col")), P(None, ("row", "col")), P())
    return jax.shard_map(shards, mesh=mesh, in_specs=in_specs, out_specs=out_specs, check_vma=False)
```

time: 203 us -> 64.9 us (0.32)
  the two profiles are of different devices: /device:TPU:32 before, /device:TPU:1 now
where the time goes in v1:
time: 64.9 us; the launch traced here: 64.2 us
  Pallas kernels  55.1 us (85%)
  local copies, waits for them, and re-layouts  8.4 us (13%)
    pallas_call x1, Pallas kernels, shards(): pl.pallas_call(kernel, out_shape=[jax.ShapeDtypeStruct((32, 128), F32)] *...  55.1 us
    unnamed x4, local copies, waits for them, and re-layouts  8.4 us

profile of v1, /device:TPU:1, one launch (start us, length us, event | category | flops | bytes accessed | tf_op | source)
XLA Modules:
  0.0 64.2 jit_solution(5509366830231710503)
XLA Ops:
  0.6 55.1 %average_and_update.1 = (f32[32,128]{1,0:T(8,128)}, f32[32,128]{1,0:T(8,128)}, f32[32,128]{1,0:T(8,128)}, bf16[4,4,4,2,2,32,128]{6,5,4,3,2,1,0:T(8,128)(2,1)}) custom-call(bf16[4,4,4,2,2,32,128]{6,5,4,3,2,1,0:T(8,128)(2,1)} %bitcast.40, f32[32,128]{1,0:T(8,128)} %bitcast.42, f32[32,128]{1,0:T(8,128)} %bitcast.43, f32[32,128]{1,0:T(8,128)} %bitcast.44), custom_call_target="tpu_custom_call" | custom-call | tf_op jit(solution)/shard_map/average_and_update/pallas_call | solution.py:315
  55.8 1.3 %copy.20 = f32[2,2048]{1,0:T(2,128)} copy(f32[2,2048]{1,0:T(2,128)} %bitcast.47) | data formatting | bytes 32768
  57.1 1.3 %copy.21 = f32[2,2048]{1,0:T(2,128)} copy(f32[2,2048]{1,0:T(2,128)} %bitcast.46) | data formatting | bytes 32768
  58.4 1.3 %copy.22 = f32[2,2048]{1,0:T(2,128)} copy(f32[2,2048]{1,0:T(2,128)} %bitcast.45) | data formatting | bytes 32768
  59.7 4.4 %copy.23 = bf16[2,524288]{1,0:T(2,128)(2,1)} copy(bf16[2,524288]{1,0:T(2,128)(2,1)} %bitcast.41) | data formatting | bytes 4194304
